TPU v7x, 512 devices: a whole 4x8x8 slice. The times are simulated.
512 devices in a mesh: batch: 16 (over z_lo, x, core), seq: 32 (over y, z_hi).
Axes of the slice: x: 4, y: 8, z: 8 (z_hi: 4, z_lo: 2; z = z_hi * 2 + z_lo), core: 2. Of those that a mesh axis runs over, the one named last changes fastest.
Arguments:
- layer_inputs: bfloat16 [409600, 800], P(('batch', 'seq')), may hold values from -24 to 24
- output_grads: bfloat16 [409600, 800], P(('batch', 'seq')), may hold values from -48 to 48
- input_inverse: float32 [800, 200], replicated, may hold values from -1 to 3
- output_inverse: float32 [800, 200], replicated, may hold values from -1 to 3
Outputs:
- input_factor: float32 [800, 200], P('seq')
- output_factor: float32 [800, 200], P('seq')
- preconditioned: bfloat16 [800, 800], replicated
All inputs are finite; a program needn't handle non-finite values.
Results may differ from a plain program's by a relative error of at most 0.0075.
Values may be sent and summed in bfloat16 or wider, within the bound.
A program may use at most 64 MiB of HBM per device.

v0:
```python
import jax
import jax.numpy as jnp
from jax import lax
from jax.sharding import Mesh
from jax.sharding import PartitionSpec as P

BLOCK = 200
SEQ = ("seq_0", "seq_1")
BATCH_SEQ = ("batch", "seq_0", "seq_1")


def scatter_axes(x, axes, dim):
    if not axes:
        return x
    nearer = lax.psum_scatter(x, axes[0], scatter_dimension=dim, tiled=True)
    return scatter_axes(nearer, axes[1:], dim)


def sent_to_all(x, axis):
    peers = lax.axis_size(axis)
    return lax.all_to_all(jnp.broadcast_to(x[None], (peers, *x.shape)), axis, 0, 0, tiled=True)


def taken_together(x, axis):
    return sent_to_all(x, axis).sum(axis=0)


def together(arrays, axis):
    ends = [0]
    for a in arrays:
        ends.append(ends[-1] + a.size)
    subtotal = taken_together(jnp.concatenate([a.ravel() for a in arrays]), axis)
    return tuple((subtotal[b:e].reshape(a.shape) for a, b, e in zip(arrays, ends, ends[1:])))


def block_terms(values):
    tok_rows, width = values.shape
    stacked = values.reshape(tok_rows, width // BLOCK, BLOCK)
    product = jnp.einsum("tnb,tnc->nbc", stacked, stacked, preferred_element_type=jnp.float32)
    return product.reshape(width, BLOCK)


def reduce_terms(input_term, output_term, grad_term):
    shares = (
        scatter_axes(input_term.astype(jnp.bfloat16), SEQ, 0).astype(jnp.float32),
        scatter_axes(output_term.astype(jnp.bfloat16), SEQ, 0).astype(jnp.float32),
        scatter_axes(grad_term.astype(jnp.bfloat16), SEQ, 0).astype(jnp.float32),
    )
    return together((shares[0], shares[1], shares[2]), "batch")


def shards(layer_inputs, output_grads, input_inverse, output_inverse):
    tok_rows, in_width = layer_inputs.shape
    out_width = output_grads.shape[1]
    in_blocks = in_width // BLOCK
    out_blocks = out_width // BLOCK
    total_rows = tok_rows * lax.axis_size("batch") * lax.axis_size(SEQ)
    inverse_count = 1.0 / total_rows
    input_term = block_terms(layer_inputs)
    output_term = block_terms(output_grads)
    input_stack = input_inverse.reshape(in_blocks, BLOCK, BLOCK)
    output_stack = output_inverse.reshape(out_blocks, BLOCK, BLOCK)
    grad_term = lax.dot_general(
        layer_inputs, output_grads, (((0,), (0,)), ((), ())), preferred_element_type=jnp.float32
    )
    input_sum, output_sum, grad_sum = reduce_terms(input_term, output_term, grad_term)
    grad_owned = grad_sum * inverse_count
    owned_rows = grad_owned.shape[0]
    right_done = jnp.einsum(
        "rmk,mkl->rml",
        grad_owned.reshape(owned_rows, out_blocks, BLOCK),
        output_stack,
        precision=lax.Precision.HIGHEST,
    ).reshape(owned_rows, out_width)
    gathered = lax.all_gather(right_done, SEQ, axis=0, tiled=True)
    applied = jnp.einsum(
        "nij,njo->nio",
        input_stack,
        gathered.reshape(in_blocks, BLOCK, out_width),
        precision=lax.Precision.HIGHEST,
    ).reshape(in_width, out_width)
    preconditioned = applied.astype(jnp.bfloat16)
    input_factor = input_sum * inverse_count
    output_factor = output_sum * inverse_count
    return (input_factor, output_factor, preconditioned)


def solution(mesh):
    finer = Mesh(mesh.devices.reshape(mesh.shape["batch"], 8, 4), ("batch", "seq_0", "seq_1"))
    in_specs = (P(BATCH_SEQ, None), P(BATCH_SEQ, None), P(), P())
    out_specs = (P(SEQ, None), P(SEQ, None), P())
    return jax.shard_map(
        shards, mesh=finer, in_specs=in_specs, out_specs=out_specs, check_vma=False
    )
```

profile of v0, /device:TPU:2, one launch (start us, length us, event | category | flops | bytes accessed | tf_op | source)
XLA Modules:
  0.0 250.9 jit_solution(5033083344006876032)
XLA Ops:
  7.2 2.8 %copy.31 = bf16[800,800]{0,1:T(8,128)(2,1)S(1)} copy(bf16[800,800]{1,0:T(8,128)(2,1)} %param.4) | data formatting | bytes 2560000 | tf_op args[0]
  9.9 2.8 %copy.32 = bf16[800,800]{0,1:T(8,128)(2,1)S(1)} copy(bf16[800,800]{1,0:T(8,128)(2,1)} %param.5) | data formatting | bytes 2560000 | tf_op args[1]
  12.7 4.8 %convolution_convert_fusion.1 = bf16[800,800]{1,0:T(8,128)(2,1)} fusion(bf16[800,800]{1,0:T(8,128)(2,1)} %param.4, bf16[800,800]{1,0:T(8,128)(2,1)} %param.5), kind=kOutput, calls=%fused_computation.1 | convolution fusion | flops 1024640000 | bytes 3840000 | tf_op jit(solution)/shard_map/dot_general | solution.py:63
  18.7 34.1 %fusion.7 = (bf16[104,200]{1,0:T(8,128)(2,1)S(1)}, bf16[104,200]{1,0:T(8,128)(2,1)S(1)}, bf16[112,800]{1,0:T(8,128)(2,1)S(1)}) fusion(bf16[800,200]{1,0:T(8,128)(2,1)S(1)} %bitcast.40, bf16[800,200]{1,0:T(8,128)(2,1)S(1)} %bitcast.41, bf16[800,800]{1,0:T(8,128)(2,1)} %convolution_convert_fusion.1), kind=kCustom, calls=%all-reduce-scatter.6 | all-reduce-scatter fusion | flops 1049602 | bytes 2184448
  52.8 2.6 %collective-permute-start = (bf16[28,200]{1,0:T(8,128)(2,1)S(1)}, bf16[28,200]{1,0:T(8,128)(2,1)S(1)}, u32[]{:S(2)}, u32[]{:S(2)}) collective-permute-start(bf16[28,200]{1,0:T(8,128)(2,1)S(1)} %slice.31), channel_id=1, source_target_pairs={{0,4},{4,8},{8,12},{12,16},{16,20},{20,24},{24,28},{1,5},{5,9},{9,... | collective-permute-start | bytes 33608
  55.4 1.9 collective-permute-start.2
  57.4 3.4 %collective-permute-start.4 = (bf16[84,800]{1,0:T(8,128)(2,1)S(1)}, bf16[84,800]{1,0:T(8,128)(2,1)S(1)}, u32[]{:S(2)}, u32[]{:S(2)}) collective-permute-start(bf16[84,800]{1,0:T(8,128)(2,1)S(1)} %slice.35), channel_id=1, source_target_pairs={{0,4},{4,8},{8,12},{12,16},{16,20},{20,24},{24,28},{1,5},{5,9},{9,... | collective-permute-start | bytes 403208
  60.8 1.3 dynamic-slice.14
  64.6 21.1 %fusion.8 = (bf16[32,200]{1,0:T(8,128)(2,1)S(1)}, bf16[32,200]{1,0:T(8,128)(2,1)S(1)}, bf16[32,800]{1,0:T(8,128)(2,1)S(1)}) fusion(bf16[100,200]{1,0:T(8,128)(2,1)S(1)} %constant_dynamic-slice_fusion.5, bf16[100,200]{1,0:T(8,128)(2,1)S(1)} %constant_dynamic-slice_fusion.3, bf16[100,800]{1,0:T(8,128)(2,1)S(1)} %constant_dynamic-slice_fusion.1), kind=kCustom, calls=%all-reduce-scatter.7 | all-reduce-scatter fusion | flops 153601 | bytes 318848
  85.8 1.5 collective-permute-start.1
  87.3 1.3 dynamic-slice.18
  89.3 5.6 %collective-permute-start.3 = (bf16[21,200]{1,0:T(8,128)(2,1)S(1)}, bf16[21,200]{1,0:T(8,128)(2,1)S(1)}, u32[]{:S(2)}, u32[]{:S(2)}) collective-permute-start(bf16[21,200]{1,0:T(8,128)(2,1)S(1)} %slice.34), channel_id=1, source_target_pairs={{0,1},{1,2},{2,3},{4,5},{5,6},{6,7},{8,9},{9,10},{10,11},{12,13},{... | collective-permute-start | bytes 25208
  94.9 3.3 %collective-permute-start.5 = (bf16[21,800]{1,0:T(8,128)(2,1)S(1)}, bf16[21,800]{1,0:T(8,128)(2,1)S(1)}, u32[]{:S(2)}, u32[]{:S(2)}) collective-permute-start(bf16[21,800]{1,0:T(8,128)(2,1)S(1)} %slice.36), channel_id=1, source_target_pairs={{0,1},{1,2},{2,3},{4,5},{5,6},{6,7},{8,9},{9,10},{10,11},{12,13},{... | collective-permute-start | bytes 100808
  98.9 1.0 collective-permute-done.5
  100.5 2.3 broadcast_in_dim.2
  102.7 5.5 %all-to-all-start = ((f32[16,1,30000]{2,1,0:T(1,128)}), f32[16,1,30000]{2,1,0:T(1,128)S(1)}, u32[]{:S(2)}, u32[]{:S(2)}) async-start(f32[16,1,30000]{2,1,0:T(1,128)} %broadcast_in_dim.2), calls=%async_computation | async-start | bytes 3850240 | tf_op jit(solution)/shard_map/all_to_all | solution.py:21
  108.7 24.1 %all-to-all-done = f32[16,1,30000]{2,1,0:T(1,128)S(1)} async-done(((f32[16,1,30000]{2,1,0:T(1,128)}), f32[16,1,30000]{2,1,0:T(1,128)S(1)}, u32[]{:S(2)}, u32[]{:S(2)}) %all-to-all-start) | async-done | bytes 1920032 | tf_op jit(solution)/shard_map/all_to_all | solution.py:21
  132.8 1.2 reduce_sum.9
  135.0 0.8 reshape.84
  135.8 1.2 copy.39
  137.0 0.7 mul.23
  138.5 98.1 %all-gather.3.cloned.1.call-done = f32[32,25,800]{2,1,0:T(8,128)} async-done(((f32[1,25,800]{2,1,0:T(8,128)}), f32[32,25,800]{2,1,0:T(8,128)}) %all-gather.3.cloned.1.call-update) | async-done | bytes 2560016 | tf_op jit(solution)/shard_map/all_gather | solution.py:75
  236.5 2.2 reshape.82
  238.8 5.3 %convolution_convert_fusion = bf16[4,800,200]{1,2,0:T(8,128)(2,1)} fusion(f32[4,200,800]{2,1,0:T(8,128)S(1)} %reshape.82, f32[4,200,200]{2,1,0:T(8,128)} %bitcast.38), kind=kOutput, calls=%fused_computation | convolution fusion | flops 1536640000 | bytes 4480000 | tf_op jit(solution)/shard_map/nij,njo->nio/dot_general | solution.py:76
  (42 shorter events, 5.9 us)
Async XLA Ops:
  52.8 10.6 %collective-permute-start = (bf16[28,200]{1,0:T(8,128)(2,1)S(1)}, bf16[28,200]{1,0:T(8,128)(2,1)S(1)}, u32[]{:S(2)}, u32[]{:S(2)}) collective-permute-start(bf16[28,200]{1,0:T(8,128)(2,1)S(1)} %slice.31), channel_id=1, source_target_pairs={{0,4},{4,8},{8,12},{12,16},{16,20},{20,24},{24,28},{1,5},{5,9},{9,... | collective-permute-start | bytes 33608
  55.4 8.2 %collective-permute-start.2 = (bf16[28,200]{1,0:T(8,128)(2,1)S(1)}, bf16[28,200]{1,0:T(8,128)(2,1)S(1)}, u32[]{:S(2)}, u32[]{:S(2)}) collective-permute-start(bf16[28,200]{1,0:T(8,128)(2,1)S(1)} %slice.33), channel_id=1, source_target_pairs={{0,4},{4,8},{8,12},{12,16},{16,20},{20,24},{24,28},{1,5},{5,9},{9,... | collective-permute-start | bytes 33608
  57.4 6.5 %collective-permute-start.4 = (bf16[84,800]{1,0:T(8,128)(2,1)S(1)}, bf16[84,800]{1,0:T(8,128)(2,1)S(1)}, u32[]{:S(2)}, u32[]{:S(2)}) collective-permute-start(bf16[84,800]{1,0:T(8,128)(2,1)S(1)} %slice.35), channel_id=1, source_target_pairs={{0,4},{4,8},{8,12},{12,16},{16,20},{20,24},{24,28},{1,5},{5,9},{9,... | collective-permute-start | bytes 403208
  85.8 12.4 %collective-permute-start.1 = (bf16[21,200]{1,0:T(8,128)(2,1)S(1)}, bf16[21,200]{1,0:T(8,128)(2,1)S(1)}, u32[]{:S(2)}, u32[]{:S(2)}) collective-permute-start(bf16[21,200]{1,0:T(8,128)(2,1)S(1)} %slice.32), channel_id=1, source_target_pairs={{0,1},{1,2},{2,3},{4,5},{5,6},{6,7},{8,9},{9,10},{10,11},{12,13},{... | collective-permute-start | bytes 25208
  89.3 9.1 %collective-permute-start.3 = (bf16[21,200]{1,0:T(8,128)(2,1)S(1)}, bf16[21,200]{1,0:T(8,128)(2,1)S(1)}, u32[]{:S(2)}, u32[]{:S(2)}) collective-permute-start(bf16[21,200]{1,0:T(8,128)(2,1)S(1)} %slice.34), channel_id=1, source_target_pairs={{0,1},{1,2},{2,3},{4,5},{5,6},{6,7},{8,9},{9,10},{10,11},{12,13},{... | collective-permute-start | bytes 25208
  94.9 5.0 %collective-permute-start.5 = (bf16[21,800]{1,0:T(8,128)(2,1)S(1)}, bf16[21,800]{1,0:T(8,128)(2,1)S(1)}, u32[]{:S(2)}, u32[]{:S(2)}) collective-permute-start(bf16[21,800]{1,0:T(8,128)(2,1)S(1)} %slice.36), channel_id=1, source_target_pairs={{0,1},{1,2},{2,3},{4,5},{5,6},{6,7},{8,9},{9,10},{10,11},{12,13},{... | collective-permute-start | bytes 100808
  102.7 5.7 %copy-start = (f32[800,200]{0,1:T(8,128)S(1)}, f32[800,200]{0,1:T(8,128)}, u32[]{:S(2)}) copy-start(f32[800,200]{0,1:T(8,128)} %param.7) | copy-start | bytes 1920004
  102.7 30.1 %all-to-all-start = ((f32[16,1,30000]{2,1,0:T(1,128)}), f32[16,1,30000]{2,1,0:T(1,128)S(1)}, u32[]{:S(2)}, u32[]{:S(2)}) async-start(f32[16,1,30000]{2,1,0:T(1,128)} %broadcast_in_dim.2), calls=%async_computation | async-start | bytes 3850240 | tf_op jit(solution)/shard_map/all_to_all | solution.py:21
  108.2 128.3 %all-gather.3.cloned.1.call-start = ((), (), s32[]{:S(2)}) async-start(), calls=%async_computation.1 | async-start | bytes 3784704 | tf_op jit(solution)/shard_map/all_gather | solution.py:75
  134.0 1.8 copy-start.1
Sparse Core Ops, SparseCore 0:
  135.9 100.5 all-gather.2
where the time goes:
time: 251 us
  waiting for transfers between devices  123 us (49%)
  blocking collectives  55.2 us (22%)
  starting transfers between devices  24 us (10%)
  local copies, waits for them, and re-layouts  18.9 us (8%)
  between operations  16.4 us (7%)
  matrix products  11.8 us (5%)
    all_gather x1, waiting for transfers between devices, shards(): gathered = lax.all_gather(right_done, SEQ, axis=0, tiled=True)  98.1 us
    unnamed x2, blocking collectives  55.2 us
    all_to_all x1, waiting for transfers between devices, sent_to_all(): lax.all_to_all(jnp.broadcast_to(x[None], (peers, *x.shape)), axis, 0, 0,...  24.1 us
    unnamed x6, starting transfers between devices  18.3 us
    unnamed x27, local copies, waits for them, and re-layouts  10.8 us
    all_to_all x1, starting transfers between devices, sent_to_all(): lax.all_to_all(jnp.broadcast_to(x[None], (peers, *x.shape)), axis, 0, 0,...  5.46 us
    dot_general x1, matrix products, shards(): jnp.einsum('nij,njo->nio', input_stack, gathered.reshape(in_blocks, BLOCK...  5.26 us
  transfers between devices with their start and end apart: 8, of which 3 were waited for; matrix products, arithmetic and copies ran while one was open for 3% of the time, Pallas kernels for 0%

commit v1 on v0

--- a/solution.py
+++ b/solution.py
@@ -72,7 +72,9 @@
         output_stack,
         precision=lax.Precision.HIGHEST,
     ).reshape(owned_rows, out_width)
-    gathered = lax.all_gather(right_done, SEQ, axis=0, tiled=True)
+    gathered = jnp.concatenate(
+        lax.all_to_all(jnp.stack([right_done] * lax.axis_size(SEQ)), SEQ, 0, 0), axis=0
+    )
     applied = jnp.einsum(
         "nij,njo->nio",
         input_stack,

time: 251 us -> 273 us (1.088)
  the two profiles are of different devices: /device:TPU:2 before, /device:TPU:350 now
where the time goes in v1:
time: 273 us
  waiting for transfers between devices  155 us (57%)
  blocking collectives  46.6 us (17%)
  starting transfers between devices  34.7 us (13%)
  local copies, waits for them, and re-layouts  20.4 us (7%)
  matrix products  11.8 us (4%)
  between operations  2.94 us (1%)
    all_to_all x1, waiting for transfers between devices, shards(): lax.all_to_all(jnp.stack([right_done] * lax.axis_size(SEQ)), SEQ, 0, 0)  122 us
    unnamed x2, blocking collectives  46.6 us
    all_to_all x1, waiting for transfers between devices, sent_to_all(): lax.all_to_all(jnp.broadcast_to(x[None], (peers, *x.shape)), axis, 0, 0,...  25.6 us
    unnamed x6, starting transfers between devices  17 us
    all_to_all x1, starting transfers between devices, shards(): lax.all_to_all(jnp.stack([right_done] * lax.axis_size(SEQ)), SEQ, 0, 0)  11.9 us
    unnamed x26, local copies, waits for them, and re-layouts  9.94 us
    unnamed x6, waiting for transfers between devices  7.14 us
    all_to_all x1, starting transfers between devices, sent_to_all(): lax.all_to_all(jnp.broadcast_to(x[None], (peers, *x.shape)), axis, 0, 0,...  5.81 us
  transfers between devices with their start and end apart: 8, of which 5 were waited for; matrix products, arithmetic and copies ran while one was open for 2% of the time, Pallas kernels for 0%

profile of v1, /device:TPU:350, one launch (start us, length us, event | category | flops | bytes accessed | tf_op | source)
XLA Modules:
  0.0 272.6 jit_solution(17172507324947263709)
XLA Ops:
  0.6 2.8 %copy.31 = bf16[800,800]{0,1:T(8,128)(2,1)S(1)} copy(bf16[800,800]{1,0:T(8,128)(2,1)} %param.4) | data formatting | bytes 2560000 | tf_op args[0]
  3.4 2.8 %copy.32 = bf16[800,800]{0,1:T(8,128)(2,1)S(1)} copy(bf16[800,800]{1,0:T(8,128)(2,1)} %param.5) | data formatting | bytes 2560000 | tf_op args[1]
  6.1 4.8 %convolution_convert_fusion.1 = bf16[800,800]{1,0:T(8,128)(2,1)} fusion(bf16[800,800]{1,0:T(8,128)(2,1)} %param.4, bf16[800,800]{1,0:T(8,128)(2,1)} %param.5), kind=kOutput, calls=%fused_computation.1 | convolution fusion | flops 1024640000 | bytes 3840000 | tf_op jit(solution)/shard_map/dot_general | solution.py:63
  12.2 31.6 %fusion.7 = (bf16[104,200]{1,0:T(8,128)(2,1)S(1)}, bf16[104,200]{1,0:T(8,128)(2,1)S(1)}, bf16[112,800]{1,0:T(8,128)(2,1)S(1)}) fusion(bf16[800,200]{1,0:T(8,128)(2,1)S(1)} %bitcast.40, bf16[800,200]{1,0:T(8,128)(2,1)S(1)} %bitcast.41, bf16[800,800]{1,0:T(8,128)(2,1)} %convolution_convert_fusion.1), kind=kCustom, calls=%all-reduce-scatter.6 | all-reduce-scatter fusion | flops 1049602 | bytes 2184448
  43.7 5.6 %collective-permute-start = (bf16[28,200]{1,0:T(8,128)(2,1)S(1)}, bf16[28,200]{1,0:T(8,128)(2,1)S(1)}, u32[]{:S(2)}, u32[]{:S(2)}) collective-permute-start(bf16[28,200]{1,0:T(8,128)(2,1)S(1)} %slice.31), channel_id=1, source_target_pairs={{0,4},{4,8},{8,12},{12,16},{16,20},{20,24},{24,28},{1,5},{5,9},{9,... | collective-permute-start | bytes 33608
  49.4 1.9 collective-permute-start.2
  51.3 2.8 %collective-permute-start.4 = (bf16[84,800]{1,0:T(8,128)(2,1)S(1)}, bf16[84,800]{1,0:T(8,128)(2,1)S(1)}, u32[]{:S(2)}, u32[]{:S(2)}) collective-permute-start(bf16[84,800]{1,0:T(8,128)(2,1)S(1)} %slice.35), channel_id=1, source_target_pairs={{0,4},{4,8},{8,12},{12,16},{16,20},{20,24},{24,28},{1,5},{5,9},{9,... | collective-permute-start | bytes 403208
  54.1 1.3 dynamic-slice.14
  57.2 1.3 collective-permute-done.4
  59.2 15.1 %fusion.8 = (bf16[32,200]{1,0:T(8,128)(2,1)S(1)}, bf16[32,200]{1,0:T(8,128)(2,1)S(1)}, bf16[32,800]{1,0:T(8,128)(2,1)S(1)}) fusion(bf16[100,200]{1,0:T(8,128)(2,1)S(1)} %constant_dynamic-slice_fusion.5, bf16[100,200]{1,0:T(8,128)(2,1)S(1)} %constant_dynamic-slice_fusion.3, bf16[100,800]{1,0:T(8,128)(2,1)S(1)} %constant_dynamic-slice_fusion.1), kind=kCustom, calls=%all-reduce-scatter.7 | all-reduce-scatter fusion | flops 153601 | bytes 318848
  74.3 2.9 %collective-permute-start.1 = (bf16[21,200]{1,0:T(8,128)(2,1)S(1)}, bf16[21,200]{1,0:T(8,128)(2,1)S(1)}, u32[]{:S(2)}, u32[]{:S(2)}) collective-permute-start(bf16[21,200]{1,0:T(8,128)(2,1)S(1)} %slice.32), channel_id=1, source_target_pairs={{0,1},{1,2},{2,3},{4,5},{5,6},{6,7},{8,9},{9,10},{10,11},{12,13},{... | collective-permute-start | bytes 25208
  77.2 1.3 dynamic-slice.18
  79.1 1.9 collective-permute-start.3
  81.1 1.9 collective-permute-start.5
  83.2 3.6 %collective-permute-done.3 = bf16[21,200]{1,0:T(8,128)(2,1)S(1)} collective-permute-done((bf16[21,200]{1,0:T(8,128)(2,1)S(1)}, bf16[21,200]{1,0:T(8,128)(2,1)S(1)}, u32[]{:S(2)}, u32[]{:S(2)}) %collective-permute-start.3) | collective-permute-done | bytes 8432
  87.2 2.2 collective-permute-done.5
  90.0 2.3 broadcast_in_dim.2
  92.3 5.8 %all-to-all-start = ((f32[16,1,30000]{2,1,0:T(1,128)}), f32[16,1,30000]{2,1,0:T(1,128)S(1)}, u32[]{:S(2)}, u32[]{:S(2)}) async-start(f32[16,1,30000]{2,1,0:T(1,128)} %broadcast_in_dim.2), calls=%async_computation | async-start | bytes 3850240 | tf_op jit(solution)/shard_map/all_to_all | solution.py:21
  98.4 25.6 %all-to-all-done = f32[16,1,30000]{2,1,0:T(1,128)S(1)} async-done(((f32[16,1,30000]{2,1,0:T(1,128)}), f32[16,1,30000]{2,1,0:T(1,128)S(1)}, u32[]{:S(2)}, u32[]{:S(2)}) %all-to-all-start) | async-done | bytes 1920032 | tf_op jit(solution)/shard_map/all_to_all | solution.py:21
  126.3 2.3 stack.3
  128.5 11.9 %all-to-all-start.1 = ((f32[32,25,800]{2,1,0:T(8,128)}), f32[32,25,800]{2,1,0:T(8,128)}, u32[]{:S(2)}, u32[]{:S(2)}) async-start(f32[32,25,800]{2,1,0:T(8,128)} %stack.3), calls=%async_computation.1 | async-start | bytes 7340032 | tf_op jit(solution)/shard_map/all_to_all | solution.py:76
  143.1 122.0 %all-to-all-done.1 = f32[32,25,800]{2,1,0:T(8,128)} async-done(((f32[32,25,800]{2,1,0:T(8,128)}), f32[32,25,800]{2,1,0:T(8,128)}, u32[]{:S(2)}, u32[]{:S(2)}) %all-to-all-start.1) | async-done | bytes 2560032 | tf_op jit(solution)/shard_map/all_to_all | solution.py:76
  265.1 2.2 reshape_reshape.3
  267.4 5.3 %convolution_convert_fusion = bf16[4,800,200]{1,2,0:T(8,128)(2,1)} fusion(f32[4,200,800]{2,1,0:T(8,128)S(1)} %reshape_reshape.3, f32[4,200,200]{2,1,0:T(8,128)} %bitcast.38), kind=kOutput, calls=%fused_computation | convolution fusion | flops 1536640000 | bytes 4480000 | tf_op jit(solution)/shard_map/nij,njo->nio/dot_general | solution.py:78
  (42 shorter events, 8.8 us)
Async XLA Ops:
  43.7 12.9 %collective-permute-start = (bf16[28,200]{1,0:T(8,128)(2,1)S(1)}, bf16[28,200]{1,0:T(8,128)(2,1)S(1)}, u32[]{:S(2)}, u32[]{:S(2)}) collective-permute-start(bf16[28,200]{1,0:T(8,128)(2,1)S(1)} %slice.31), channel_id=1, source_target_pairs={{0,4},{4,8},{8,12},{12,16},{16,20},{20,24},{24,28},{1,5},{5,9},{9,... | collective-permute-start | bytes 33608
  49.4 7.6 %collective-permute-start.2 = (bf16[28,200]{1,0:T(8,128)(2,1)S(1)}, bf16[28,200]{1,0:T(8,128)(2,1)S(1)}, u32[]{:S(2)}, u32[]{:S(2)}) collective-permute-start(bf16[28,200]{1,0:T(8,128)(2,1)S(1)} %slice.33), channel_id=1, source_target_pairs={{0,4},{4,8},{8,12},{12,16},{16,20},{20,24},{24,28},{1,5},{5,9},{9,... | collective-permute-start | bytes 33608
  51.3 7.1 %collective-permute-start.4 = (bf16[84,800]{1,0:T(8,128)(2,1)S(1)}, bf16[84,800]{1,0:T(8,128)(2,1)S(1)}, u32[]{:S(2)}, u32[]{:S(2)}) collective-permute-start(bf16[84,800]{1,0:T(8,128)(2,1)S(1)} %slice.35), channel_id=1, source_target_pairs={{0,4},{4,8},{8,12},{12,16},{16,20},{20,24},{24,28},{1,5},{5,9},{9,... | collective-permute-start | bytes 403208
  74.3 8.7 %collective-permute-start.1 = (bf16[21,200]{1,0:T(8,128)(2,1)S(1)}, bf16[21,200]{1,0:T(8,128)(2,1)S(1)}, u32[]{:S(2)}, u32[]{:S(2)}) collective-permute-start(bf16[21,200]{1,0:T(8,128)(2,1)S(1)} %slice.32), channel_id=1, source_target_pairs={{0,1},{1,2},{2,3},{4,5},{5,6},{6,7},{8,9},{9,10},{10,11},{12,13},{... | collective-permute-start | bytes 25208
  79.1 7.7 %collective-permute-start.3 = (bf16[21,200]{1,0:T(8,128)(2,1)S(1)}, bf16[21,200]{1,0:T(8,128)(2,1)S(1)}, u32[]{:S(2)}, u32[]{:S(2)}) collective-permute-start(bf16[21,200]{1,0:T(8,128)(2,1)S(1)} %slice.34), channel_id=1, source_target_pairs={{0,1},{1,2},{2,3},{4,5},{5,6},{6,7},{8,9},{9,10},{10,11},{12,13},{... | collective-permute-start | bytes 25208
  81.1 8.4 %collective-permute-start.5 = (bf16[21,800]{1,0:T(8,128)(2,1)S(1)}, bf16[21,800]{1,0:T(8,128)(2,1)S(1)}, u32[]{:S(2)}, u32[]{:S(2)}) collective-permute-start(bf16[21,800]{1,0:T(8,128)(2,1)S(1)} %slice.36), channel_id=1, source_target_pairs={{0,1},{1,2},{2,3},{4,5},{5,6},{6,7},{8,9},{9,10},{10,11},{12,13},{... | collective-permute-start | bytes 100808
  92.3 5.8 %copy-start = (f32[800,200]{0,1:T(8,128)S(1)}, f32[800,200]{0,1:T(8,128)}, u32[]{:S(2)}) copy-start(f32[800,200]{0,1:T(8,128)} %param.7) | copy-start | bytes 1920004
  92.3 31.7 %all-to-all-start = ((f32[16,1,30000]{2,1,0:T(1,128)}), f32[16,1,30000]{2,1,0:T(1,128)S(1)}, u32[]{:S(2)}, u32[]{:S(2)}) async-start(f32[16,1,30000]{2,1,0:T(1,128)} %broadcast_in_dim.2), calls=%async_computation | async-start | bytes 3850240 | tf_op jit(solution)/shard_map/all_to_all | solution.py:21
  128.5 11.9 %copy-start.1 = (f32[800,200]{0,1:T(8,128)S(1)}, f32[800,200]{0,1:T(8,128)}, u32[]{:S(2)}) copy-start(f32[800,200]{0,1:T(8,128)} %param.6) | copy-start | bytes 1920004
  128.5 136.6 %all-to-all-start.1 = ((f32[32,25,800]{2,1,0:T(8,128)}), f32[32,25,800]{2,1,0:T(8,128)}, u32[]{:S(2)}, u32[]{:S(2)}) async-start(f32[32,25,800]{2,1,0:T(8,128)} %stack.3), calls=%async_computation.1 | async-start | bytes 7340032 | tf_op jit(solution)/shard_map/all_to_all | solution.py:76
